TPU v7x, 32 devices: a whole 2x2x4 slice. The times are simulated.
32 devices in a mesh: view: 4 (over x, core), gauss: 8 (over z, y).
Axes of the slice: x: 2, y: 2, z: 4, core: 2. Of those that a mesh axis runs over, the one named last changes fastest.
Arguments:
- means: float32 [3, 131072], P(None, 'gauss'), may hold values from -1 to 1
- scales: float32 [3, 131072], P(None, 'gauss'), may hold values from 0.05 to 0.6
- quats: float32 [4, 131072], P(None, 'gauss'), may hold values from -6 to 6
- attrs: float32 [49, 131072], P(None, 'gauss'), may hold values from -6 to 6
- grad_screen: float32 [16, 2, 131072], P('view', None, 'gauss'), may hold values from -6 to 6
- visible: int32 [16, 131072], P('view', 'gauss'), may hold values 0 or 1
- clone_mask: int32 [131072], P('gauss'), may hold values from 0 to 1, as said below
- rotation: float32 [16, 3, 3], P('view'), may hold values from -3.5 to 3.5
- shift: float32 [16, 3], P('view'), may hold values from 2 to 5
- focal: float32 [16], P('view'), may hold values from 1 to 4
Outputs:
- peak_stats: float32 [2, 131072], P(None, 'gauss')
- clones: float32 [61, 131072], P(None, 'gauss')
- clone_total: int32 [], replicated
Inputs may be any that keep to these rules, and one draw needn't show every extreme that they name: `clone_mask`: in every draw some shard of 16384 consecutive Gaussians has all of them marked.
All inputs are finite; a program needn't handle non-finite values. No bound on the sum of `visible` on one device may be relied on, other than what follows from the above.
Results may differ from a plain program's by a relative error of at most 0.0003.
Values sent between devices are 32-bit elements; how exact they have to be, the bound alone decides.
A program may use at most 128 MiB of HBM per device.

v0:
```python
import jax
import jax.numpy as jnp
from jax import lax
from jax.sharding import PartitionSpec as P

G_DEV = 16384


def entering(value, axis, join, neutral):
    count, mine = (lax.axis_size(axis), lax.axis_index(axis))
    pieces = lax.all_gather(value, axis)
    running = jnp.full_like(value, 0) + jnp.asarray(neutral, value.dtype)

    def step(position, running):
        longer = join(running, pieces[position])
        return jnp.where(position < mine, longer, running)

    return lax.fori_loop(0, count - 1, step, running)


def quat_factor(scales, quats):
    inv = 1.0 / jnp.sqrt(jnp.sum(quats * quats, axis=0) + 0.25)
    w, x, y, z = (quats[0] * inv, quats[1] * inv, quats[2] * inv, quats[3] * inv)
    rq = [
        [1 - 2 * (y * y + z * z), 2 * (x * y - w * z), 2 * (x * z + w * y)],
        [2 * (x * y + w * z), 1 - 2 * (x * x + z * z), 2 * (y * z - w * x)],
        [2 * (x * z - w * y), 2 * (y * z + w * x), 1 - 2 * (x * x + y * y)],
    ]
    return [[rq[i][j] * scales[j] for j in range(3)] for i in range(3)]


def view_stats(means, factor, grad, seen, rot, trans, focal_v):
    point = [
        rot[i, 0] * means[0] + rot[i, 1] * means[1] + rot[i, 2] * means[2] + trans[i]
        for i in range(3)
    ]
    depth = jnp.maximum(point[2], 1.0)
    j00 = focal_v / depth
    j02 = -focal_v * point[0] / (depth * depth)
    j12 = -focal_v * point[1] / (depth * depth)
    first = [j00 * rot[0, j] + j02 * rot[2, j] for j in range(3)]
    second = [j00 * rot[1, j] + j12 * rot[2, j] for j in range(3)]
    prow = [sum((first[j] * factor[j][k] for j in range(3))) for k in range(3)]
    qrow = [sum((second[j] * factor[j][k] for j in range(3))) for k in range(3)]
    a_val = prow[0] ** 2 + prow[1] ** 2 + prow[2] ** 2 + 0.3
    c_val = qrow[0] ** 2 + qrow[1] ** 2 + qrow[2] ** 2 + 0.3
    b_val = prow[0] * qrow[0] + prow[1] * qrow[1] + prow[2] * qrow[2]
    half = 0.5 * (a_val - c_val)
    lam = 0.5 * (a_val + c_val) + jnp.sqrt(half * half + b_val * b_val + 0.01)
    seenf = seen.astype(jnp.float32)
    radius = 3.0 * jnp.sqrt(lam) * seenf
    gnorm = jnp.sqrt(grad[0] * grad[0] + grad[1] * grad[1]) * seenf
    return (gnorm, radius)


def add_ints(earlier, later):
    return earlier + later


def body(means, scales, quats, attrs, grad_screen, visible, clone_mask, rotation, shift, focal):
    factor = quat_factor(scales, quats)
    gmax = jnp.zeros(means.shape[1], jnp.float32)
    rmax = jnp.zeros(means.shape[1], jnp.float32)
    for v in range(grad_screen.shape[0]):
        gnorm, radius = view_stats(
            means, factor, grad_screen[v], visible[v], rotation[v], shift[v], focal[v]
        )
        gmax = jnp.maximum(gmax, gnorm)
        rmax = jnp.maximum(rmax, radius)
    gmax, rmax = lax.pmax((gmax, rmax), "view")
    peak = jnp.stack([gmax, rmax])
    rows = jnp.concatenate([means, scales, quats, attrs, peak], axis=0)
    feat_rows = rows.shape[0]
    shards = lax.axis_size("gauss")
    cap_blk = G_DEV // 128
    count = jnp.sum(clone_mask)
    blocks = (count + 127) // 128
    offset = entering(blocks, "gauss", add_ints, jnp.int32(0))
    summed = lax.psum(count.astype(jnp.float32), "gauss")
    total = summed.astype(jnp.int32)
    rank = jnp.cumsum(clone_mask) - 1
    where_to = jnp.where(clone_mask == 1, rank, cap_blk * 128)
    packed = (
        jnp.zeros((feat_rows, cap_blk * 128), jnp.float32).at[:, where_to].set(rows, mode="drop")
    )
    packed = packed.reshape(feat_rows, cap_blk, 128)
    per = (cap_blk + shards - 1) // shards
    target = jnp.arange(shards, dtype=jnp.int32)[:, None]
    within = jnp.arange(per, dtype=jnp.int32)[None, :]
    local_blk = (target - offset) % shards + within * shards
    valid = local_blk < blocks
    picked = jnp.minimum(local_blk, cap_blk - 1).reshape(-1)
    outgoing = packed[:, picked, :] * valid.reshape(1, -1, 1).astype(jnp.float32)
    outgoing = outgoing.reshape(feat_rows, shards, per, 128)
    slot_ids = (
        jnp.where(valid, (offset + local_blk) // shards, cap_blk)
        .astype(jnp.int32)
        .reshape(1, shards, per)
    )
    width = 128 // lax.axis_size("view")
    start = lax.axis_index("view") * width
    portion = lax.dynamic_slice_in_dim(outgoing, start, width, 3)
    arrived, slots_in = (
        lax.all_to_all(portion, "gauss", split_axis=1, concat_axis=1, tiled=True),
        lax.all_to_all(slot_ids, "gauss", split_axis=1, concat_axis=1, tiled=True),
    )
    arrived = arrived.reshape(feat_rows, shards * per, width)
    partial_place = (
        jnp.zeros((feat_rows, cap_blk, width), jnp.float32)
        .at[:, slots_in.reshape(-1)]
        .set(arrived, mode="drop")
    )
    placed = lax.all_gather(partial_place, "view", axis=2, tiled=True)
    clones = placed.reshape(feat_rows, cap_blk * 128)
    return (peak, clones, total)


def solution(mesh):
    return jax.shard_map(
        body,
        mesh=mesh,
        in_specs=(
            P(None, "gauss"),
            P(None, "gauss"),
            P(None, "gauss"),
            P(None, "gauss"),
            P("view", None, "gauss"),
            P("view", "gauss"),
            P("gauss"),
            P("view", None, None),
            P("view", None),
            P("view"),
        ),
        out_specs=(P(None, "gauss"), P(None, "gauss"), P()),
        check_vma=False,
    )
```

profile of v0, /device:TPU:0, one launch (start us, length us, event | category | flops | bytes accessed | tf_op | source)
XLA Modules:
  0.0 360.1 jit_solution(10346555730215635345)
XLA Ops:
  7.2 1.0 copy.21
  8.9 1.5 compare_select_fusion
  11.1 1.2 dynamic-slice
  12.4 0.8 dynamic-update-slice
  13.1 13.1 %all-reduce = s32[8]{0:T(128)S(1)} all-reduce(s32[8]{0:T(128)S(1)} %dynamic-update-slice), channel_id=1, replica_groups=mesh['view'=4,'gauss'=8] {'gauss'}, use_global_device_ids=true, to_apply=%add | all-reduce | flops 8 | bytes 64
  26.2 8.9 %while.13 = (s32[]{:T(128)}, s32[]{:T(128)}, s32[]{:T(128)}, s32[8]{0:T(128)S(1)}, s32[]{:T(128)}) while((s32[]{:T(128)}, s32[]{:T(128)}, s32[]{:T(128)}, s32[8]{0:T(128)S(1)}, s32[]{:T(128)}) %tuple.130), condition=%wide.region_5.6_spmd, body=%wide.region_4.5_spmd.sunk | while | flops 5 | bytes 107 | solution.py:18
  35.1 0.7 compare_select_fusion.1
  35.8 3.3 all-to-all-start
  39.2 1.7 fusion.6
  40.9 1.1 multiply_reduce_fusion
  42.1 0.8 fusion.8
  42.9 0.7 fusion.9
  43.6 1.8 fusion.10
  45.4 1.5 fusion.14
  47.5 7.4 %multiply_add_fusion.23 = (f32[1,16384]{1,0:T(1,128)S(1)}, f32[1,16384]{1,0:T(1,128)S(1)}, f32[1,16384]{1,0:T(1,128)S(1)}, f32[1,16384]{1,0:T(1,128)S(1)}) fusion(f32[]{:T(128)} %bitcast.15, f32[]{:T(128)} %bitcast.11, f32[]{:T(128)} %bitcast.18, f32[3,16384]{1,0:T(4,128)} %param.12, f32[]{:T(128)} %bitcast.17, f32[]{:T(128)} %bitcast.16, f32[]{:T(128)S(6)} %neg.16, ...), kind=kLoop, calls=%fused_computation.34 | loop fusion | flops 327680 | bytes 458792 | tf_op jit(solution)/shard_map/add | solution.py:41
  54.9 7.5 %multiply_add_fusion.22 = (f32[1,16384]{1,0:T(1,128)S(1)}, f32[1,16384]{1,0:T(1,128)S(1)}, f32[1,16384]{1,0:T(1,128)S(1)}, f32[1,16384]{1,0:T(1,128)S(1)}) fusion(f32[1,16384]{1,0:T(1,128)S(1)} %get-tuple-element.103, f32[1,16384]{1,0:T(1,128)S(1)} %get-tuple-element.104, f32[]{:T(128)} %bitcast.16, f32[]{:T(128)} %bitcast.12, f32[]{:T(128)} %bitcast.13, ...), kind=kLoop, calls=%fused_computation.33 | loop fusion | flops 294912 | bytes 655400 | tf_op jit(solution)/shard_map/add | solution.py:41
  62.4 2.7 multiply_add_fusion.19
  65.0 0.7 fusion.11
  66.4 7.5 %multiply_add_fusion.17 = (f32[1,16384]{1,0:T(1,128)S(1)}, f32[1,16384]{1,0:T(1,128)S(1)}, f32[1,16384]{1,0:T(1,128)S(1)}, f32[1,16384]{1,0:T(1,128)S(1)}) fusion(f32[]{:T(128)} %bitcast.41, f32[]{:T(128)} %bitcast.37, f32[]{:T(128)} %bitcast.44, f32[3,16384]{1,0:T(4,128)} %param.12, f32[]{:T(128)} %bitcast.43, f32[]{:T(128)} %bitcast.42, f32[]{:T(128)S(6)} %neg.17, ...), kind=kLoop, calls=%fused_computation.28 | loop fusion | flops 327680 | bytes 458792 | tf_op jit(solution)/shard_map/add | solution.py:41
  73.8 6.1 %multiply_add_fusion.16 = (f32[1,16384]{1,0:T(1,128)S(1)}, f32[1,16384]{1,0:T(1,128)S(1)}, f32[1,16384]{1,0:T(1,128)S(1)}, f32[1,16384]{1,0:T(1,128)S(1)}) fusion(f32[1,16384]{1,0:T(1,128)S(1)} %get-tuple-element.109, f32[1,16384]{1,0:T(1,128)S(1)} %get-tuple-element.110, f32[]{:T(128)} %bitcast.42, f32[]{:T(128)} %bitcast.38, f32[]{:T(128)} %bitcast.39, ...), kind=kLoop, calls=%fused_computation.27 | loop fusion | flops 294912 | bytes 655400 | tf_op jit(solution)/shard_map/add | solution.py:41
  79.9 2.7 multiply_add_fusion.13
  82.7 0.7 fusion.12
  84.1 6.3 %multiply_add_fusion.11 = (f32[1,16384]{1,0:T(1,128)S(1)}, f32[1,16384]{1,0:T(1,128)S(1)}, f32[1,16384]{1,0:T(1,128)S(1)}, f32[1,16384]{1,0:T(1,128)S(1)}) fusion(f32[]{:T(128)} %bitcast.60, f32[]{:T(128)} %bitcast.56, f32[]{:T(128)} %bitcast.63, f32[3,16384]{1,0:T(4,128)S(1)} %copy-done.1, f32[]{:T(128)} %bitcast.62, f32[]{:T(128)} %bitcast.61, ...), kind=kLoop, calls=%fused_computation.22 | loop fusion | flops 327680 | bytes 458792 | tf_op jit(solution)/shard_map/add | solution.py:41
  90.4 6.1 %multiply_add_fusion.10 = (f32[1,16384]{1,0:T(1,128)S(1)}, f32[1,16384]{1,0:T(1,128)S(1)}, f32[1,16384]{1,0:T(1,128)S(1)}, f32[1,16384]{1,0:T(1,128)S(1)}) fusion(f32[1,16384]{1,0:T(1,128)S(1)} %get-tuple-element.115, f32[1,16384]{1,0:T(1,128)S(1)} %get-tuple-element.116, f32[]{:T(128)} %bitcast.61, f32[]{:T(128)} %bitcast.57, f32[]{:T(128)} %bitcast.58, ...), kind=kLoop, calls=%fused_computation.21 | loop fusion | flops 294912 | bytes 655400 | tf_op jit(solution)/shard_map/add | solution.py:41
  96.4 2.6 multiply_add_fusion.7
  99.0 0.7 fusion.13
  100.3 6.1 %multiply_add_fusion.5 = (f32[1,16384]{1,0:T(1,128)S(1)}, f32[1,16384]{1,0:T(1,128)S(1)}, f32[1,16384]{1,0:T(1,128)S(1)}, f32[1,16384]{1,0:T(1,128)S(1)}) fusion(f32[]{:T(128)} %bitcast.79, f32[]{:T(128)} %bitcast.75, f32[]{:T(128)} %bitcast.82, f32[3,16384]{1,0:T(4,128)S(1)} %copy-done.1, f32[]{:T(128)} %bitcast.81, f32[]{:T(128)} %bitcast.80, f32[]{:T(128)S(6)} %neg.19, ...), kind=kLoop, calls=%fused_computation.16 | loop fusion | flops 327680 | bytes 458792 | tf_op jit(solution)/shard_map/add | solution.py:41
  106.3 6.2 %multiply_add_fusion.4 = (f32[1,16384]{1,0:T(1,128)S(1)}, f32[1,16384]{1,0:T(1,128)S(1)}, f32[1,16384]{1,0:T(1,128)S(1)}, f32[1,16384]{1,0:T(1,128)S(1)}) fusion(f32[1,16384]{1,0:T(1,128)S(1)} %get-tuple-element.121, f32[1,16384]{1,0:T(1,128)S(1)} %get-tuple-element.122, f32[]{:T(128)} %bitcast.80, f32[]{:T(128)} %bitcast.76, f32[]{:T(128)} %bitcast.77, ...), kind=kLoop, calls=%fused_computation.15 | loop fusion | flops 294912 | bytes 655400 | tf_op jit(solution)/shard_map/add | solution.py:41
  112.5 2.6 multiply_add_fusion.1
  115.4 0.8 add_sqrt_fusion.3
  116.9 1.4 multiply_maximum_fusion
  118.6 33.1 %all-reduce.4.cloned.1.call-done = (f32[1,16384]{1,0:T(1,128)}, f32[1,16384]{1,0:T(1,128)}) async-done(((f32[1,16384]{1,0:T(1,128)}, f32[1,16384]{1,0:T(1,128)}), (f32[1,16384]{1,0:T(1,128)}, f32[1,16384]{1,0:T(1,128)})) %all-reduce.4.cloned.1.call-update) | async-done | bytes 131088 | tf_op jit(solution)/shard_map/pmax | solution.py:70
  151.7 21.6 %concatenate.4 = f32[61,16384]{1,0:T(8,128)} concatenate(f32[3,16384]{1,0:T(4,128)S(1)} %copy-done.1, f32[3,16384]{1,0:T(4,128)S(1)} %copy-done.3, f32[4,16384]{1,0:T(4,128)S(1)} %copy-done.2, f32[49,16384]{1,0:T(8,128)} %param.15, f32[1,16384]{1,0:T(1,128)} %get-tuple-element.101, f32[1,16384]{1,0:T(1,128)} %get-tuple-element.100), dimensions={0} | concatenate | bytes 7995392 | tf_op jit(solution)/shard_map/concatenate | solution.py:72
  173.2 6.9 %copy.24 = f32[16384,61]{1,0:T(8,128)} copy(f32[16384,61]{0,1:T(8,128)} %bitcast.130) | data formatting | bytes 7995392 | tf_op jit(solution)/shard_map/concatenate | solution.py:72
  180.1 44.4 %scatter_custom_fusion = f32[61,16384]{0,1:T(8,128)} fusion(s32[16384]{0:T(1024)S(1)} %get-tuple-element.157, f32[16384,61]{1,0:T(8,128)} %copy.24, f32[]{:T(128)} %constant.86.clone.1), kind=kCustom, calls=%fused_computation.3 | custom fusion | bytes 3998208 | tf_op jit(solution)/shard_map/scatter | solution.py:84
  224.5 7.7 %gather_fusion = f32[128,61,128]{1,2,0:T(8,128)} fusion(f32[61,128,128]{0,2,1:T(8,128)} %bitcast.128, s32[1024]{0:T(1024)S(1)} %pad_clamp_fusion), kind=kCustom, calls=%fused_computation | custom fusion | bytes 7995904 | tf_op jit(solution)/shard_map/gather | solution.py:93
  232.2 1.8 fusion.15
  234.0 3.9 %reshape.632 = f32[8,1,31232]{2,1,0:T(1,128)} reshape(f32[8,16,32,61]{3,2,1,0:T(8,128)S(1)} %fusion.15) | data formatting | bytes 1998848
  237.9 5.5 %all-to-all-start.1 = ((f32[8,1,31232]{2,1,0:T(1,128)}), f32[8,1,31232]{2,1,0:T(1,128)S(1)}, u32[]{:S(2)}, u32[]{:S(2)}) async-start(f32[8,1,31232]{2,1,0:T(1,128)} %reshape.632), calls=%async_computation.1 | async-start | bytes 1998848 | tf_op jit(solution)/shard_map/all_to_all | solution.py:104
  244.8 22.6 %all-to-all-done.1 = f32[8,1,31232]{2,1,0:T(1,128)S(1)} async-done(((f32[8,1,31232]{2,1,0:T(1,128)}), f32[8,1,31232]{2,1,0:T(1,128)S(1)}, u32[]{:S(2)}, u32[]{:S(2)}) %all-to-all-start.1) | async-done | bytes 999456 | tf_op jit(solution)/shard_map/all_to_all | solution.py:104
  267.9 3.0 reduce.6
  270.9 4.3 %reshape.633 = f32[8,16,32,61]{3,2,1,0:T(8,128)} reshape(f32[8,31232]{1,0:T(8,128)S(1)} %reduce.6) | data formatting | bytes 1998848
  275.5 12.0 %scatter_fusion = f32[61,128,32]{0,2,1:T(8,128)S(1)} fusion(f32[61,128,32]{0,2,1:T(8,128)S(1)} %broadcast_in_dim.21, s32[128]{0:T(128)S(1)} %fusion.4, f32[128,61,32]{1,2,0:T(8,128)} %bitcast.129), kind=kCustom, calls=%fused_computation.2 | custom fusion | bytes 2998784 | tf_op jit(solution)/shard_map/scatter | solution.py:111
  287.5 1.3 copy-done
  289.4 19.8 %psum.7 = f32[]{:T(128)} all-reduce(f32[]{:T(128)S(6)} %convert_element_type.47), channel_id=1, replica_groups=mesh['view'=4,'gauss'=8] {'gauss'}, use_global_device_ids=true, to_apply=%region_10.11 | all-reduce | flops 1 | bytes 8 | tf_op jit(solution)/shard_map/psum | solution.py:79
  309.9 0.8 pad_maximum_fusion
  310.7 34.7 %all-gather.2.cloned.1.call-done = f32[61,128,128]{0,2,1:T(8,128)} async-done(((f32[61,128,32]{0,2,1:T(8,128)}), f32[61,128,128]{0,2,1:T(8,128)}) %all-gather.2.cloned.1.call-update) | async-done | bytes 3997712 | tf_op jit(solution)/shard_map/all_gather | solution.py:113
  345.3 6.8 %copy.25 = f32[61,16384]{1,0:T(8,128)} copy(f32[61,16384]{0,1:T(8,128)} %bitcast.131) | data formatting | bytes 7995392
  (53 shorter events, 8.4 us)
Async XLA Ops:
  7.2 66.7 %copy-start.1 = (f32[3,16384]{1,0:T(4,128)S(1)}, f32[3,16384]{1,0:T(4,128)}, u32[]{:S(2)}) copy-start(f32[3,16384]{1,0:T(4,128)} %param.12) | copy-start | bytes 589828
  7.2 107.9 %copy-start.7 = (s32[4,16384]{1,0:T(4,128)S(1)}, s32[4,16384]{1,0:T(4,128)}, u32[]{:S(2)}) copy-start(s32[4,16384]{1,0:T(4,128)} %param.17) | copy-start | bytes 786436
  8.2 107.1 %copy-start.3 = (f32[3,16384]{1,0:T(4,128)S(1)}, f32[3,16384]{1,0:T(4,128)}, u32[]{:S(2)}) copy-start(f32[3,16384]{1,0:T(4,128)} %param.13) | copy-start | bytes 589828
  8.8 106.7 %copy-start.4 = (f32[4,2,16384]{2,1,0:T(2,128)S(1)}, f32[4,2,16384]{2,1,0:T(2,128)}, u32[]{:S(2)}) copy-start(f32[4,2,16384]{2,1,0:T(2,128)} %param.16) | copy-start | bytes 1572868
  35.8 202.1 %all-to-all-start = ((s32[1,8,16]{2,0,1:T(1,128)}), s32[1,8,16]{2,0,1:T(1,128)S(1)}, u32[]{:S(2)}, u32[]{:S(2)}) async-start(s32[1,8,16]{2,0,1:T(1,128)} %compare_select_fusion.1), calls=%async_computation | async-start | bytes 8192 | tf_op jit(solution)/shard_map/all_to_all | solution.py:105
  39.1 112.5 %all-reduce.4.cloned.1.call-start = ((), (), s32[]{:S(2)}) async-start(), calls=%async_computation.3 | async-start | bytes 262144 | tf_op jit(solution)/shard_map/pmax | solution.py:70
  79.9 71.7 %copy-start.2 = (f32[4,16384]{1,0:T(4,128)S(1)}, f32[4,16384]{1,0:T(4,128)}, u32[]{:S(2)}) copy-start(f32[4,16384]{1,0:T(4,128)} %param.14) | copy-start | bytes 786436
  237.9 29.4 %all-to-all-start.1 = ((f32[8,1,31232]{2,1,0:T(1,128)}), f32[8,1,31232]{2,1,0:T(1,128)S(1)}, u32[]{:S(2)}, u32[]{:S(2)}) async-start(f32[8,1,31232]{2,1,0:T(1,128)} %reshape.632), calls=%async_computation.1 | async-start | bytes 1998848 | tf_op jit(solution)/shard_map/all_to_all | solution.py:104
  243.5 101.9 %all-gather.2.cloned.1.call-start = ((), (), s32[]{:S(2)}) async-start(), calls=%async_computation.2 | async-start | bytes 10485760 | tf_op jit(solution)/shard_map/all_gather | solution.py:113
  275.4 34.4 %copy-start.5 = (f32[1,16384]{1,0:T(1,128)S(1)}, f32[1,16384]{1,0:T(1,128)}, u32[]{:S(2)}) copy-start(f32[1,16384]{1,0:T(1,128)} %get-tuple-element.100) | copy-start | bytes 196612
  275.4 34.4 %copy-start.6 = (f32[1,16384]{1,0:T(1,128)S(1)}, f32[1,16384]{1,0:T(1,128)}, u32[]{:S(2)}) copy-start(f32[1,16384]{1,0:T(1,128)} %get-tuple-element.101) | copy-start | bytes 196612
  287.5 1.3 copy-start
Sparse Core Ops, SparseCore 0:
  118.4 33.1 all-reduce.3
  288.9 56.3 all-gather.1
where the time goes:
time: 363 us; the launch traced here: 360 us
  local copies, waits for them, and re-layouts  127 us (35%)
  waiting for transfers between devices  90.4 us (25%)
  other arithmetic  76.7 us (21%)
  blocking collectives  32.9 us (9%)
  between operations  19.9 us (5%)
  starting transfers between devices  8.9 us (2%)
  loops' own time  4.58 us (1%)
    add x8, other arithmetic, view_stats(): first = [j00 * rot[0, j] + j02 * rot[2, j] for j in range(3)]  53 us
    scatter x1, local copies, waits for them, and re-layouts, body(): jnp.zeros((feat_rows, cap_blk * 128), jnp.float32).at[:, where_to]  44.4 us
    all_gather x1, waiting for transfers between devices, body(): placed = lax.all_gather(partial_place, 'view', axis=2, tiled=True)  34.7 us
    pmax x1, waiting for transfers between devices, body(): gmax, rmax = lax.pmax((gmax, rmax), 'view')  33.1 us
    concatenate x2, local copies, waits for them, and re-layouts, body(): rows = jnp.concatenate([means, scales, quats, attrs, peak], axis=0)  28.5 us
    all_to_all x1, waiting for transfers between devices, body(): lax.all_to_all(portion, 'gauss', split_axis=1, concat_axis=1, tiled=True)  22.6 us
    psum x1, blocking collectives, body(): summed = lax.psum(count.astype(jnp.float32), 'gauss')  19.8 us
    unnamed x24, local copies, waits for them, and re-layouts  18.4 us
  transfers between devices with their start and end apart: 4, of which 3 were waited for; matrix products, arithmetic and copies ran while one was open for 46% of the time, Pallas kernels for 0%

commit v1 on v0

--- a/solution.py
+++ b/solution.py
@@ -110,7 +110,7 @@
         .at[:, slots_in.reshape(-1)]
         .set(arrived, mode="drop")
     )
-    placed = lax.all_gather(partial_place, "view", axis=2, tiled=True)
+    placed = jnp.concatenate(lax.all_gather(partial_place, "view"), axis=2)
     clones = placed.reshape(feat_rows, cap_blk * 128)
     return (peak, clones, total)
 

time: 363 us -> 348 us (0.959)
  waiting for transfers between devices: 90.4 us -> 65.4 us
  local copies, waits for them, and re-layouts: 127 us -> 137 us
    all_gather x1, waiting for transfers between devices: 34.7 us -> 9.74 us  [body(): placed = jnp.concatenate(lax.all_gather(partial_place, 'view'), axis=2)]
    reshape x1 -> x2, local copies, waits for them, and re-layouts: 0.98 us -> 10.3 us  [the longest x1 9.28 us: body(): placed = jnp.concatenate(lax.all_gather(partial_place, 'view'), axis=2)]
    scatter x1 -> x2, local copies, waits for them, and re-layouts: 12 us -> 14.6 us  [body(): partial_place = jnp.zeros((feat_rows, cap_blk, width), jnp.float32).at[:,...]
    unnamed x24 -> x22, local copies, waits for them, and re-layouts: 18.4 us -> 17.1 us
  transfers between devices with their start and end apart: 4 -> 4, of which waited for: 3 -> 3; matrix products, arithmetic and copies ran while one was open for 46% -> 48% of each run, Pallas kernels for 0% -> 0%
where the time goes in v1:
time: 348 us; the launch traced here: 345 us
  local copies, waits for them, and re-layouts  137 us (39%)
  other arithmetic  76.8 us (22%)
  waiting for transfers between devices  65.4 us (19%)
  blocking collectives  32.9 us (9%)
  between operations  20 us (6%)
  starting transfers between devices  8.92 us (3%)
  loops' own time  4.1 us (1%)
    add x8, other arithmetic, view_stats(): first = [j00 * rot[0, j] + j02 * rot[2, j] for j in range(3)]  52.7 us
    scatter x1, local copies, waits for them, and re-layouts, body(): jnp.zeros((feat_rows, cap_blk * 128), jnp.float32).at[:, where_to]  44.3 us
    pmax x1, waiting for transfers between devices, body(): gmax, rmax = lax.pmax((gmax, rmax), 'view')  33.1 us
    concatenate x2, local copies, waits for them, and re-layouts, body(): rows = jnp.concatenate([means, scales, quats, attrs, peak], axis=0)  28.5 us
    all_to_all x1, waiting for transfers between devices, body(): lax.all_to_all(portion, 'gauss', split_axis=1, concat_axis=1, tiled=True)  22.6 us
    psum x1, blocking collectives, body(): summed = lax.psum(count.astype(jnp.float32), 'gauss')  19.8 us
    unnamed x22, local copies, waits for them, and re-layouts  17.1 us
    scatter x2, local copies, waits for them, and re-layouts, body(): partial_place = jnp.zeros((feat_rows, cap_blk, width), jnp.float32).at[:,...  14.6 us
  transfers between devices with their start and end apart: 4, of which 3 were waited for; matrix products, arithmetic and copies ran while one was open for 48% of the time, Pallas kernels for 0%

profile of v1, /device:TPU:0, one launch (start us, length us, event | category | flops | bytes accessed | tf_op | source)
XLA Modules:
  0.0 345.2 jit_solution(12069117192737252019)
XLA Ops:
  7.2 1.0 copy.23
  8.9 1.6 compare_select_fusion
  11.2 1.2 dynamic-slice
  12.4 0.8 dynamic-update-slice
  13.2 13.1 %all-reduce = s32[8]{0:T(128)S(1)} all-reduce(s32[8]{0:T(128)S(1)} %dynamic-update-slice), channel_id=1, replica_groups=mesh['view'=4,'gauss'=8] {'gauss'}, use_global_device_ids=true, to_apply=%add | all-reduce | flops 8 | bytes 64
  26.2 8.2 %while.13 = (s32[]{:T(128)}, s32[]{:T(128)}, s32[]{:T(128)}, s32[8]{0:T(128)S(1)}, s32[]{:T(128)}) while((s32[]{:T(128)}, s32[]{:T(128)}, s32[]{:T(128)}, s32[8]{0:T(128)S(1)}, s32[]{:T(128)}) %tuple.129), condition=%wide.region_5.6_spmd, body=%wide.region_4.5_spmd.sunk | while | flops 5 | bytes 107 | solution.py:18
  34.5 0.7 compare_select_fusion.1
  35.2 3.3 all-to-all-start
  38.5 1.7 fusion.6
  40.3 1.1 multiply_reduce_fusion
  41.4 0.8 fusion.8
  42.3 0.7 fusion.9
  43.0 1.8 fusion.10
  44.8 1.5 fusion.14
  46.9 7.4 %multiply_add_fusion.23 = (f32[1,16384]{1,0:T(1,128)S(1)}, f32[1,16384]{1,0:T(1,128)S(1)}, f32[1,16384]{1,0:T(1,128)S(1)}, f32[1,16384]{1,0:T(1,128)S(1)}) fusion(f32[]{:T(128)} %bitcast.15, f32[]{:T(128)} %bitcast.11, f32[]{:T(128)} %bitcast.18, f32[3,16384]{1,0:T(4,128)} %param.12, f32[]{:T(128)} %bitcast.17, f32[]{:T(128)} %bitcast.16, f32[]{:T(128)S(6)} %neg.16, ...), kind=kLoop, calls=%fused_computation.34 | loop fusion | flops 327680 | bytes 458792 | tf_op jit(solution)/shard_map/add | solution.py:41
  54.3 7.4 %multiply_add_fusion.22 = (f32[1,16384]{1,0:T(1,128)S(1)}, f32[1,16384]{1,0:T(1,128)S(1)}, f32[1,16384]{1,0:T(1,128)S(1)}, f32[1,16384]{1,0:T(1,128)S(1)}) fusion(f32[1,16384]{1,0:T(1,128)S(1)} %get-tuple-element.100, f32[1,16384]{1,0:T(1,128)S(1)} %get-tuple-element.101, f32[]{:T(128)} %bitcast.16, f32[]{:T(128)} %bitcast.12, f32[]{:T(128)} %bitcast.13, ...), kind=kLoop, calls=%fused_computation.33 | loop fusion | flops 294912 | bytes 655400 | tf_op jit(solution)/shard_map/add | solution.py:41
  61.7 2.7 multiply_add_fusion.19
  64.4 0.7 fusion.11
  65.7 7.4 %multiply_add_fusion.17 = (f32[1,16384]{1,0:T(1,128)S(1)}, f32[1,16384]{1,0:T(1,128)S(1)}, f32[1,16384]{1,0:T(1,128)S(1)}, f32[1,16384]{1,0:T(1,128)S(1)}) fusion(f32[]{:T(128)} %bitcast.41, f32[]{:T(128)} %bitcast.37, f32[]{:T(128)} %bitcast.44, f32[3,16384]{1,0:T(4,128)} %param.12, f32[]{:T(128)} %bitcast.43, f32[]{:T(128)} %bitcast.42, f32[]{:T(128)S(6)} %neg.17, ...), kind=kLoop, calls=%fused_computation.28 | loop fusion | flops 327680 | bytes 458792 | tf_op jit(solution)/shard_map/add | solution.py:41
  73.1 6.2 %multiply_add_fusion.16 = (f32[1,16384]{1,0:T(1,128)S(1)}, f32[1,16384]{1,0:T(1,128)S(1)}, f32[1,16384]{1,0:T(1,128)S(1)}, f32[1,16384]{1,0:T(1,128)S(1)}) fusion(f32[1,16384]{1,0:T(1,128)S(1)} %get-tuple-element.106, f32[1,16384]{1,0:T(1,128)S(1)} %get-tuple-element.107, f32[]{:T(128)} %bitcast.42, f32[]{:T(128)} %bitcast.38, f32[]{:T(128)} %bitcast.39, ...), kind=kLoop, calls=%fused_computation.27 | loop fusion | flops 294912 | bytes 655400 | tf_op jit(solution)/shard_map/add | solution.py:41
  79.4 2.8 multiply_add_fusion.13
  83.5 6.1 %multiply_add_fusion.11 = (f32[1,16384]{1,0:T(1,128)S(1)}, f32[1,16384]{1,0:T(1,128)S(1)}, f32[1,16384]{1,0:T(1,128)S(1)}, f32[1,16384]{1,0:T(1,128)S(1)}) fusion(f32[]{:T(128)} %bitcast.60, f32[]{:T(128)} %bitcast.56, f32[]{:T(128)} %bitcast.63, f32[3,16384]{1,0:T(4,128)S(1)} %copy-done, f32[]{:T(128)} %bitcast.62, f32[]{:T(128)} %bitcast.61, f32[]{:T(128)S(6)} %neg.18, ...), kind=kLoop, calls=%fused_computation.22 | loop fusion | flops 327680 | bytes 458792 | tf_op jit(solution)/shard_map/add | solution.py:41
  89.6 6.1 %multiply_add_fusion.10 = (f32[1,16384]{1,0:T(1,128)S(1)}, f32[1,16384]{1,0:T(1,128)S(1)}, f32[1,16384]{1,0:T(1,128)S(1)}, f32[1,16384]{1,0:T(1,128)S(1)}) fusion(f32[1,16384]{1,0:T(1,128)S(1)} %get-tuple-element.112, f32[1,16384]{1,0:T(1,128)S(1)} %get-tuple-element.113, f32[]{:T(128)} %bitcast.61, f32[]{:T(128)} %bitcast.57, f32[]{:T(128)} %bitcast.58, ...), kind=kLoop, calls=%fused_computation.21 | loop fusion | flops 294912 | bytes 655400 | tf_op jit(solution)/shard_map/add | solution.py:41
  95.7 2.8 multiply_add_fusion.7
  98.5 0.7 fusion.13
  99.8 6.1 %multiply_add_fusion.5 = (f32[1,16384]{1,0:T(1,128)S(1)}, f32[1,16384]{1,0:T(1,128)S(1)}, f32[1,16384]{1,0:T(1,128)S(1)}, f32[1,16384]{1,0:T(1,128)S(1)}) fusion(f32[]{:T(128)} %bitcast.79, f32[]{:T(128)} %bitcast.75, f32[]{:T(128)} %bitcast.82, f32[3,16384]{1,0:T(4,128)S(1)} %copy-done, f32[]{:T(128)} %bitcast.81, f32[]{:T(128)} %bitcast.80, f32[]{:T(128)S(6)} %neg.19, ...), kind=kLoop, calls=%fused_computation.16 | loop fusion | flops 327680 | bytes 458792 | tf_op jit(solution)/shard_map/add | solution.py:41
  105.9 6.0 %multiply_add_fusion.4 = (f32[1,16384]{1,0:T(1,128)S(1)}, f32[1,16384]{1,0:T(1,128)S(1)}, f32[1,16384]{1,0:T(1,128)S(1)}, f32[1,16384]{1,0:T(1,128)S(1)}) fusion(f32[1,16384]{1,0:T(1,128)S(1)} %get-tuple-element.118, f32[1,16384]{1,0:T(1,128)S(1)} %get-tuple-element.119, f32[]{:T(128)} %bitcast.80, f32[]{:T(128)} %bitcast.76, f32[]{:T(128)} %bitcast.77, ...), kind=kLoop, calls=%fused_computation.15 | loop fusion | flops 294912 | bytes 655400 | tf_op jit(solution)/shard_map/add | solution.py:41
  111.9 2.7 multiply_add_fusion.1
  114.9 0.8 add_sqrt_fusion.3
  116.4 1.4 multiply_maximum_fusion
  118.0 33.1 %all-reduce.4.cloned.1.call-done = (f32[1,16384]{1,0:T(1,128)}, f32[1,16384]{1,0:T(1,128)}) async-done(((f32[1,16384]{1,0:T(1,128)}, f32[1,16384]{1,0:T(1,128)}), (f32[1,16384]{1,0:T(1,128)}, f32[1,16384]{1,0:T(1,128)})) %all-reduce.4.cloned.1.call-update) | async-done | bytes 131088 | tf_op jit(solution)/shard_map/pmax | solution.py:70
  151.1 21.6 %concatenate.4 = f32[61,16384]{1,0:T(8,128)} concatenate(f32[3,16384]{1,0:T(4,128)S(1)} %copy-done, f32[3,16384]{1,0:T(4,128)S(1)} %copy-done.2, f32[4,16384]{1,0:T(4,128)S(1)} %copy-done.1, f32[49,16384]{1,0:T(8,128)} %param.15, f32[1,16384]{1,0:T(1,128)} %get-tuple-element.98, f32[1,16384]{1,0:T(1,128)} %get-tuple-element.97), dimensions={0} | concatenate | bytes 7995392 | tf_op jit(solution)/shard_map/concatenate | solution.py:72
  172.7 6.9 %copy.26 = f32[16384,61]{1,0:T(8,128)} copy(f32[16384,61]{0,1:T(8,128)} %bitcast.134) | data formatting | bytes 7995392 | tf_op jit(solution)/shard_map/concatenate | solution.py:72
  179.6 44.3 %scatter_custom_fusion = f32[61,16384]{0,1:T(8,128)} fusion(s32[16384]{0:T(1024)S(1)} %get-tuple-element.154, f32[16384,61]{1,0:T(8,128)} %copy.26, f32[]{:T(128)} %constant.86.clone.1), kind=kCustom, calls=%fused_computation.3 | custom fusion | bytes 3998208 | tf_op jit(solution)/shard_map/scatter | solution.py:84
  223.9 7.7 %gather_fusion = f32[128,61,128]{1,2,0:T(8,128)} fusion(f32[61,128,128]{0,2,1:T(8,128)} %bitcast.132, s32[1024]{0:T(1024)S(1)} %pad_clamp_fusion), kind=kCustom, calls=%fused_computation | custom fusion | bytes 7995904 | tf_op jit(solution)/shard_map/gather | solution.py:93
  231.6 1.8 fusion.15
  233.4 3.9 %reshape.633 = f32[8,1,31232]{2,1,0:T(1,128)} reshape(f32[8,16,32,61]{3,2,1,0:T(8,128)S(1)} %fusion.15) | data formatting | bytes 1998848
  237.4 5.5 %all-to-all-start.1 = ((f32[8,1,31232]{2,1,0:T(1,128)}), f32[8,1,31232]{2,1,0:T(1,128)S(1)}, u32[]{:S(2)}, u32[]{:S(2)}) async-start(f32[8,1,31232]{2,1,0:T(1,128)} %reshape.633), calls=%async_computation.1 | async-start | bytes 1998848 | tf_op jit(solution)/shard_map/all_to_all | solution.py:104
  244.2 22.6 %all-to-all-done.1 = f32[8,1,31232]{2,1,0:T(1,128)S(1)} async-done(((f32[8,1,31232]{2,1,0:T(1,128)}), f32[8,1,31232]{2,1,0:T(1,128)S(1)}, u32[]{:S(2)}, u32[]{:S(2)}) %all-to-all-start.1) | async-done | bytes 999456 | tf_op jit(solution)/shard_map/all_to_all | solution.py:104
  267.3 3.0 reduce.6
  270.3 4.3 %reshape.634 = f32[8,16,32,61]{3,2,1,0:T(8,128)} reshape(f32[8,31232]{1,0:T(8,128)S(1)} %reduce.6) | data formatting | bytes 1998848
  274.9 12.0 %scatter_fusion = f32[61,128,32]{0,2,1:T(8,128)S(1)} fusion(f32[61,128,32]{0,2,1:T(8,128)S(1)} %broadcast_in_dim.21, s32[128]{0:T(128)S(1)} %fusion.4, f32[128,61,32]{1,2,0:T(8,128)} %bitcast.133), kind=kCustom, calls=%fused_computation.2 | custom fusion | bytes 2998784 | tf_op jit(solution)/shard_map/scatter | solution.py:111
  286.9 2.5 copy.27
  290.1 19.8 %psum.7 = f32[]{:T(128)} all-reduce(f32[]{:T(128)S(6)} %convert_element_type.47), channel_id=1, replica_groups=mesh['view'=4,'gauss'=8] {'gauss'}, use_global_device_ids=true, to_apply=%region_10.11 | all-reduce | flops 1 | bytes 8 | tf_op jit(solution)/shard_map/psum | solution.py:79
  310.5 0.8 pad_maximum_fusion
  311.3 9.7 %all-gather.3.cloned.1.call-done = f32[244,128,32]{1,2,0:T(8,128)} async-done(((f32[61,128,32]{1,2,0:T(8,128)}), f32[244,128,32]{1,2,0:T(8,128)}) %all-gather.3.cloned.1.call-update) | async-done | bytes 3997712 | tf_op jit(solution)/shard_map/all_gather | solution.py:113
  321.1 9.3 %copy.28 = f32[61,128,4,32]{0,3,2,1:T(8,128)} copy(f32[61,128,4,32]{1,3,0,2:T(8,128)} %bitcast.136) | data formatting | bytes 7995392 | tf_op jit(solution)/shard_map/reshape | solution.py:113
  330.3 6.8 %copy.29 = f32[61,16384]{1,0:T(8,128)} copy(f32[61,16384]{0,1:T(8,128)} %bitcast.131) | data formatting | bytes 7995392
  (53 shorter events, 8.9 us)
Async XLA Ops:
  7.2 65.9 %copy-start = (f32[3,16384]{1,0:T(4,128)S(1)}, f32[3,16384]{1,0:T(4,128)}, u32[]{:S(2)}) copy-start(f32[3,16384]{1,0:T(4,128)} %param.12) | copy-start | bytes 589828
  7.2 107.3 %copy-start.6 = (s32[4,16384]{1,0:T(4,128)S(1)}, s32[4,16384]{1,0:T(4,128)}, u32[]{:S(2)}) copy-start(s32[4,16384]{1,0:T(4,128)} %param.17) | copy-start | bytes 786436
  8.2 106.5 %copy-start.2 = (f32[3,16384]{1,0:T(4,128)S(1)}, f32[3,16384]{1,0:T(4,128)}, u32[]{:S(2)}) copy-start(f32[3,16384]{1,0:T(4,128)} %param.13) | copy-start | bytes 589828
  8.8 106.1 %copy-start.3 = (f32[4,2,16384]{2,1,0:T(2,128)S(1)}, f32[4,2,16384]{2,1,0:T(2,128)}, u32[]{:S(2)}) copy-start(f32[4,2,16384]{2,1,0:T(2,128)} %param.16) | copy-start | bytes 1572868
  35.2 202.2 %all-to-all-start = ((s32[1,8,16]{2,0,1:T(1,128)}), s32[1,8,16]{2,0,1:T(1,128)S(1)}, u32[]{:S(2)}, u32[]{:S(2)}) async-start(s32[1,8,16]{2,0,1:T(1,128)} %compare_select_fusion.1), calls=%async_computation | async-start | bytes 8192 | tf_op jit(solution)/shard_map/all_to_all | solution.py:105
  38.5 112.6 %all-reduce.4.cloned.1.call-start = ((), (), s32[]{:S(2)}) async-start(), calls=%async_computation.3 | async-start | bytes 262144 | tf_op jit(solution)/shard_map/pmax | solution.py:70
  79.3 71.8 %copy-start.1 = (f32[4,16384]{1,0:T(4,128)S(1)}, f32[4,16384]{1,0:T(4,128)}, u32[]{:S(2)}) copy-start(f32[4,16384]{1,0:T(4,128)} %param.14) | copy-start | bytes 786436
  237.4 29.4 %all-to-all-start.1 = ((f32[8,1,31232]{2,1,0:T(1,128)}), f32[8,1,31232]{2,1,0:T(1,128)S(1)}, u32[]{:S(2)}, u32[]{:S(2)}) async-start(f32[8,1,31232]{2,1,0:T(1,128)} %reshape.633), calls=%async_computation.1 | async-start | bytes 1998848 | tf_op jit(solution)/shard_map/all_to_all | solution.py:104
  242.9 78.2 %all-gather.3.cloned.1.call-start = ((), (), s32[]{:S(2)}) async-start(), calls=%async_computation.2 | async-start | bytes 4997120 | tf_op jit(solution)/shard_map/all_gather | solution.py:113
  274.9 35.6 %copy-start.4 = (f32[1,16384]{1,0:T(1,128)S(1)}, f32[1,16384]{1,0:T(1,128)}, u32[]{:S(2)}) copy-start(f32[1,16384]{1,0:T(1,128)} %get-tuple-element.97) | copy-start | bytes 196612
  274.9 35.6 %copy-start.5 = (f32[1,16384]{1,0:T(1,128)S(1)}, f32[1,16384]{1,0:T(1,128)}, u32[]{:S(2)}) copy-start(f32[1,16384]{1,0:T(1,128)} %get-tuple-element.98) | copy-start | bytes 196612
Sparse Core Ops, SparseCore 0:
  117.9 33.1 all-reduce.3
  289.6 31.4 all-gather.2
